TPU v7x, 32 devices: a whole 2x2x4 slice. The times are simulated.
32 devices in a mesh: section: 2 (over x), dp: 16 (over z, y, core).
Axes of the slice: x: 2, y: 2, z: 4, core: 2. Of those that a mesh axis runs over, the one named last changes fastest.
Arguments:
- features: bfloat16 [1, 2, 2048, 4096], P(None, 'section', 'dp'), parts along dimension 2, may hold values from -6 to 6
- in_proj: bfloat16 [2, 4096, 512], P('section'), may hold values from -0.09375 to 0.09375
- mix_proj: bfloat16 [2, 2, 256, 256], P('section'), may hold values from -0.375 to 0.375
- out_proj: bfloat16 [2, 512, 4096], P('section'), may hold values from -0.375 to 0.375
- gate_proj: bfloat16 [2, 2, 4096], P('section'), may hold values from -0.09375 to 0.09375
- cross_bias: float32 [2, 4096], P('section'), may hold values from -3 to 3
Outputs:
- crossed: bfloat16 [1, 2, 2048, 4096], P(None, 'section', 'dp'), parts along dimension 2
There are 16 independent parts, one for each index of `dp`. A program takes and returns all parts, laid end to end along the dimension named above; an argument that names none is the same for every part. Nothing has to cross between parts.
All inputs are finite; a program needn't handle non-finite values.
Results may differ from a plain program's by a relative error of at most 0.015.
Values may be sent and summed in bfloat16 or wider, within the bound.
A program may use at most 64 MiB of HBM per device.

v0:
```python
import jax
import jax.numpy as jnp
from jax import lax
from jax.sharding import PartitionSpec as P


def from_behind(block, axis, distance):
    devices = range(lax.axis_size(axis))
    route = [(i - distance, i) for i in devices if i - distance in devices]
    return lax.ppermute(block, axis, route)


def cross_layer(current, anchor, v_mat, c_mat, u_mat, gate_mat, shift_row):
    row_count = current.shape[0]
    expert_count = c_mat.shape[0]
    rank_size = c_mat.shape[1]
    projected = jnp.dot(current, v_mat, preferred_element_type=jnp.float32)
    inner_first = (
        jnp.tanh(projected).astype(jnp.bfloat16).reshape(row_count, expert_count, rank_size)
    )
    inner_second = jnp.einsum(
        "rek,ekj->rej", inner_first, c_mat, preferred_element_type=jnp.float32
    )
    logits = lax.dot_general(
        current, gate_mat, (((1,), (1,)), ((), ())), preferred_element_type=jnp.float32
    )
    gate_values = 1.0 / jnp.sum(jnp.exp(logits[:, None, :] - logits[:, :, None]), axis=2)
    blended = (gate_values[:, :, None] * jnp.tanh(inner_second)).astype(jnp.bfloat16)
    blended = blended.reshape(row_count, expert_count * rank_size)
    crossed = jnp.dot(blended, u_mat, preferred_element_type=jnp.float32)
    updated = current.astype(jnp.float32) + anchor.astype(jnp.float32) * (crossed + shift_row)
    return updated.astype(jnp.bfloat16)


def per_device(features, in_proj, mix_proj, out_proj, gate_proj, cross_bias):
    section_count = lax.axis_size("section")
    position = lax.axis_index("section")
    pieces = 1
    local_micro = features.shape[0]
    row_count = features.shape[2]
    feature_count = features.shape[3]
    piece_rows = row_count // pieces
    everyone = lax.all_gather(features, "section", axis=1, tiled=True)
    all_units = everyone.reshape(local_micro * section_count * pieces, piece_rows, feature_count)
    unit_count = all_units.shape[0]
    step_count = unit_count + section_count - 1
    v_mat = in_proj[0]
    c_mat = mix_proj[0]
    u_mat = out_proj[0]
    gate_mat = gate_proj[0]
    shift_row = cross_bias[0]

    def apply_layer(current, anchor):
        return cross_layer(current, anchor, v_mat, c_mat, u_mat, gate_mat, shift_row)

    def keep_input(current, anchor):
        return current

    def advance(carried, moment):
        incoming, outgoing, collected = carried
        unit_here = moment - position
        active = (unit_here >= 0) & (unit_here < unit_count)
        anchor = lax.dynamic_index_in_dim(
            all_units, jnp.clip(unit_here, 0, unit_count - 1), 0, keepdims=False
        )
        current = jnp.where(position == 0, anchor, incoming)
        result = lax.cond(active, apply_layer, keep_input, current, anchor)
        outgoing = jnp.where(position == section_count - 1, result, outgoing)
        held_unit = moment + position - 2 * section_count + 2
        arrived = (
            (held_unit >= 0)
            & (held_unit < unit_count)
            & (held_unit // pieces % section_count == position)
        )
        held_safe = jnp.clip(held_unit, 0, unit_count - 1)
        slot_index = held_safe // pieces // section_count * pieces + held_safe % pieces
        previous = lax.dynamic_index_in_dim(collected, slot_index, 0, keepdims=False)
        collected = lax.dynamic_update_index_in_dim(
            collected, jnp.where(arrived, outgoing, previous), slot_index, 0
        )
        return (result, outgoing, collected)

    def forward_step(carried, moment):
        result, outgoing, collected = advance(carried, moment)
        incoming = from_behind(result, "section", 1)
        return ((incoming, outgoing, collected), None)

    def cycle_step(carried, moment):
        moved, _ = forward_step(carried, moment)
        incoming, outgoing, collected = moved
        outgoing = from_behind(outgoing, "section", -1)
        return ((incoming, outgoing, collected), None)

    blank = jnp.zeros((piece_rows, feature_count), jnp.bfloat16)
    holding = jnp.zeros((local_micro * pieces, piece_rows, feature_count), jnp.bfloat16)
    carried, _ = lax.scan(
        forward_step, (blank, blank, holding), jnp.arange(0, section_count - 1, dtype=jnp.int32)
    )
    carried, _ = lax.scan(
        cycle_step, carried, jnp.arange(section_count - 1, step_count - 1, dtype=jnp.int32)
    )
    _, _, collected = advance(carried, jnp.int32(step_count - 1))
    return collected.reshape(local_micro, 1, row_count, feature_count)


def solution(mesh):
    placed = (
        P(None, "section", "dp", None),
        P("section", None, None),
        P("section", None, None, None),
        P("section", None, None),
        P("section", None, None),
        P("section", None),
    )
    return jax.shard_map(
        per_device,
        mesh=mesh,
        in_specs=placed,
        out_specs=P(None, "section", "dp", None),
        check_vma=False,
    )
```

profile of v0, /device:TPU:2, one launch (start us, length us, event | category | flops | bytes accessed | tf_op | source)
XLA Modules:
  0.0 130.4 jit_solution(13214571090702250396)
XLA Ops:
  6.5 0.0 all-gather.2.cloned.1.call-start
  6.5 0.0 copy-start
  6.5 0.0 copy-start.1
  6.5 0.0 copy-start.2
  6.5 0.7 all-gather.2.cloned.1.call-update
  7.3 34.8 %all-gather.2.cloned.1.call-done = bf16[1,2,128,4096]{3,2,0,1:T(8,128)(2,1)} async-done(((bf16[1,1,128,4096]{3,2,0,1:T(8,128)(2,1)}), bf16[1,2,128,4096]{3,2,0,1:T(8,128)(2,1)}) %all-gather.2.cloned.1.call-update) | async-done | bytes 2097168 | tf_op jit(solution)/shard_map/all_gather | solution.py:43
  42.1 1.4 %broadcast_select_fusion.2 = (bf16[128,4096]{1,0:T(8,128)(2,1)S(1)}, bf16[128,4096]{1,0:T(8,128)(2,1)S(1)}) fusion(pred[]{:T(512)S(6)} %eq.38, bf16[1,2,128,4096]{3,2,0,1:T(8,128)(2,1)} %all-gather.2.cloned.1.call-done, s32[]{:T(128)S(6)} %min.19), kind=kLoop, calls=%fused_computation.48 | loop fusion | flops 524288 | bytes 3145733 | tf_op jit(solution)/shard_map/while/body/eval_jaxpr/jit(_where)/select_n | solution.py:66
  43.5 0.0 copy-done
  43.5 0.0 copy-done.1
  43.5 0.0 copy-done.2
  43.5 1.3 collective-permute-start
  44.8 32.0 %collective-permute-done = bf16[128,4096]{1,0:T(8,128)(2,1)} collective-permute-done((bf16[128,4096]{1,0:T(8,128)(2,1)S(1)}, bf16[128,4096]{1,0:T(8,128)(2,1)}, u32[]{:S(2)}, u32[]{:S(2)}) %collective-permute-start) | collective-permute-done | bytes 1048608 | tf_op jit(solution)/shard_map/while/body/eval_jaxpr/ppermute | solution.py:10
  76.8 1.7 %broadcast_select_fusion.1 = (bf16[128,4096]{1,0:T(8,128)(2,1)S(1)}, bf16[128,4096]{1,0:T(8,128)(2,1)S(1)}) fusion(bf16[128,4096]{1,0:T(8,128)(2,1)} %collective-permute-done, pred[]{:T(512)S(6)} %eq.38, bf16[1,2,128,4096]{3,2,0,1:T(8,128)(2,1)} %all-gather.2.cloned.1.call-done, s32[]{:T(128)S(6)} %min.18), kind=kLoop, calls=%fused_computation.47 | loop fusion | flops 524288 | bytes 4194309 | tf_op jit(solution)/shard_map/while/body/eval_jaxpr/jit(_where)/select_n | solution.py:66
  78.5 7.3 %conditional.4 = (bf16[128,4096]{1,0:T(8,128)(2,1)S(1)}) conditional(s32[]{:T(128)} %convert_element_type.57, bf16[128,4096]{1,0:T(8,128)(2,1)S(1)} %get-tuple-element.150, (bf16[128,4096]{1,0:T(8,128)(2,1)S(1)}, bf16[128,4096]{1,0:T(8,128)(2,1)S(1)}, bf16[2,4096]{1,0:T(2,128)(2,1)S(1)}, bf16[4096,512]{1,0:T(8,128)(2,1)}, ...), branch_computations={%region_3.4_spmd, %region_4.6_spmd} | conditional | flops 1112736768 | bytes 15767588 | solution.py:67
  78.5 0.0 copy-start.3
  78.5 3.0 %fusion.14 = bf16[128,512]{1,0:T(8,128)(2,1)S(1)} fusion(bf16[128,4096]{1,0:T(8,128)(2,1)S(1)} %get-tuple-element.134, bf16[4096,512]{1,0:T(8,128)(2,1)} %get-tuple-element.137), kind=kOutput, calls=%fused_computation.22 | convolution fusion | flops 536936448 | bytes 5373952 | tf_op jit(solution)/shard_map/while/body/eval_jaxpr/cond/branch_1_fun/dot_general | solution.py:17
  81.5 0.4 fusion.28
  81.9 0.0 copy-done.3
  82.0 0.2 fusion.15
  82.2 0.1 copy.44
  82.3 3.6 %fusion.11 = bf16[128,4096]{1,0:T(8,128)(2,1)S(1)} fusion(bf16[128,512]{0,1:T(8,128)(2,1)S(1)} %bitcast.81, bf16[512,4096]{1,0:T(8,128)(2,1)} %get-tuple-element.139, bf16[128,4096]{1,0:T(8,128)(2,1)S(1)} %get-tuple-element.135, bf16[128,4096]{1,0:T(8,128)(2,1)S(1)} %get-tuple-element.134, f32[4096]{0:T(1024)S(1)} %bitcast.87), kind=kOutput, calls=%fused_computation.17 | convolution fusion | flops 540016640 | bytes 7487488 | tf_op jit(solution)/shard_map/while/body/eval_jaxpr/cond/branch_1_fun/dot_general | solution.py:30
  85.9 1.3 collective-permute-start.1
  87.2 1.1 broadcast_select_fusion.3
  88.3 6.5 %collective-permute-start.2 = (bf16[128,4096]{1,0:T(8,128)(2,1)}, bf16[128,4096]{1,0:T(8,128)(2,1)}, u32[]{:S(2)}, u32[]{:S(2)}) collective-permute-start(bf16[128,4096]{1,0:T(8,128)(2,1)} %broadcast_select_fusion.3), channel_id=1, source_target_pairs={{16,0},{17,1},{18,2},{19,3},{20,4},{21,5},{22,6},{23,7},{24,8},{25... | collective-permute-start | bytes 3145736 | tf_op jit(solution)/shard_map/while/body/eval_jaxpr/ppermute | solution.py:10
  94.8 17.2 %collective-permute-done.1 = bf16[128,4096]{1,0:T(8,128)(2,1)} collective-permute-done((bf16[128,4096]{1,0:T(8,128)(2,1)S(1)}, bf16[128,4096]{1,0:T(8,128)(2,1)}, u32[]{:S(2)}, u32[]{:S(2)}) %collective-permute-start.1) | collective-permute-done | bytes 1048608 | tf_op jit(solution)/shard_map/while/body/eval_jaxpr/ppermute | solution.py:10
  112.0 2.6 %broadcast_select_fusion = (bf16[128,4096]{1,0:T(8,128)(2,1)S(1)}, bf16[128,4096]{1,0:T(8,128)(2,1)}) fusion(bf16[128,4096]{1,0:T(8,128)(2,1)} %collective-permute-done.1, pred[]{:T(512)S(6)} %eq.38, bf16[1,2,128,4096]{3,2,0,1:T(8,128)(2,1)} %all-gather.2.cloned.1.call-done, s32[]{:T(128)S(6)} %min.17), kind=kLoop, calls=%fused_computation.46 | loop fusion | flops 524288 | bytes 4194309 | tf_op jit(solution)/shard_map/jit(_where)/select_n | solution.py:66
  114.7 7.6 %conditional.5 = (bf16[128,4096]{1,0:T(8,128)(2,1)S(1)}) conditional(s32[]{:T(128)} %convert_element_type.56, bf16[128,4096]{1,0:T(8,128)(2,1)S(1)} %get-tuple-element.148, (bf16[128,4096]{1,0:T(8,128)(2,1)S(1)}, bf16[128,4096]{1,0:T(8,128)(2,1)}, bf16[2,4096]{1,0:T(2,128)(2,1)S(1)}, bf16[4096,512]{1,0:T(8,128)(2,1)}, bf16[2,256,256]{2,1,0:T(8,128)(2,1)}, ...), branch_computations={%region_6.7_spmd, %region_7.9_spmd} | conditional | flops 1112736768 | bytes 15767588 | solution.py:67
  114.7 0.0 copy-start.4
  114.7 3.0 %fusion.23 = bf16[128,512]{1,0:T(8,128)(2,1)S(1)} fusion(bf16[128,4096]{1,0:T(8,128)(2,1)S(1)} %get-tuple-element.141, bf16[4096,512]{1,0:T(8,128)(2,1)} %get-tuple-element.144), kind=kOutput, calls=%fused_computation.36 | convolution fusion | flops 536936448 | bytes 5373952 | tf_op jit(solution)/shard_map/cond/branch_1_fun/dot_general | solution.py:17
  117.7 0.4 fusion.29
  118.1 0.0 copy-done.4
  118.1 0.2 fusion.24
  118.3 0.1 copy.46
  118.4 3.9 %fusion.20 = bf16[128,4096]{1,0:T(8,128)(2,1)S(1)} fusion(bf16[128,512]{0,1:T(8,128)(2,1)S(1)} %bitcast.82, bf16[512,4096]{1,0:T(8,128)(2,1)} %get-tuple-element.146, bf16[128,4096]{1,0:T(8,128)(2,1)} %get-tuple-element.142, bf16[128,4096]{1,0:T(8,128)(2,1)S(1)} %get-tuple-element.141, f32[4096]{0:T(1024)S(1)} %bitcast.88), kind=kOutput, calls=%fused_computation.31 | convolution fusion | flops 540016640 | bytes 7487488 | tf_op jit(solution)/shard_map/cond/branch_1_fun/dot_general | solution.py:30
  122.3 0.0 collective-permute-done.2
  122.3 1.2 select_bitcast_fusion
  (5 shorter events, 0.1 us)
Async XLA Ops:
  6.5 35.6 %all-gather.2.cloned.1.call-start = ((), (), s32[]{:S(2)}) async-start(), calls=%async_computation | async-start | bytes 3145728 | tf_op jit(solution)/shard_map/all_gather | solution.py:43
  6.5 36.9 %copy-start = (bf16[1,2,4096]{2,1,0:T(2,128)(2,1)S(1)}, bf16[1,2,4096]{2,1,0:T(2,128)(2,1)}, u32[]{:S(2)}) copy-start(bf16[1,2,4096]{2,1,0:T(2,128)(2,1)} %param.16) | copy-start | bytes 49156
  6.5 36.9 %copy-start.1 = (f32[1,4096]{1,0:T(1,128)S(1)}, f32[1,4096]{1,0:T(1,128)}, u32[]{:S(2)}) copy-start(f32[1,4096]{1,0:T(1,128)} %param.17) | copy-start | bytes 49156
  6.5 36.9 %copy-start.2 = (bf16[1,2,256,256]{3,2,1,0:T(8,128)(2,1)S(1)}, bf16[1,2,256,256]{3,2,1,0:T(8,128)(2,1)}, u32[]{:S(2)}) copy-start(bf16[1,2,256,256]{3,2,1,0:T(8,128)(2,1)} %param.14) | copy-start | bytes 786436
  43.5 33.3 %collective-permute-start = (bf16[128,4096]{1,0:T(8,128)(2,1)S(1)}, bf16[128,4096]{1,0:T(8,128)(2,1)}, u32[]{:S(2)}, u32[]{:S(2)}) collective-permute-start(bf16[128,4096]{1,0:T(8,128)(2,1)S(1)} %get-tuple-element.154), channel_id=1, source_target_pairs={{0,16},{1,17},{2,18},{3,19},{4,20},{5,21},{6,22},{7,23},{8,24},{9,... | collective-permute-start | bytes 3145736 | tf_op jit(solution)/shard_map/while/body/eval_jaxpr/ppermute | solution.py:10
  78.5 3.4 %copy-start.3 = (bf16[2,256,256]{2,1,0:T(8,128)(2,1)S(1)}, bf16[2,256,256]{2,1,0:T(8,128)(2,1)}, u32[]{:S(2)}) copy-start(bf16[2,256,256]{2,1,0:T(8,128)(2,1)} %get-tuple-element.138) | copy-start | bytes 786436 | tf_op jit(solution)/shard_map/while/body/eval_jaxpr/cond
  85.9 26.2 %collective-permute-start.1 = (bf16[128,4096]{1,0:T(8,128)(2,1)S(1)}, bf16[128,4096]{1,0:T(8,128)(2,1)}, u32[]{:S(2)}, u32[]{:S(2)}) collective-permute-start(bf16[128,4096]{1,0:T(8,128)(2,1)S(1)} %get-tuple-element.155), channel_id=1, source_target_pairs={{0,16},{1,17},{2,18},{3,19},{4,20},{5,21},{6,22},{7,23},{8,24},{9,... | collective-permute-start | bytes 3145736 | tf_op jit(solution)/shard_map/while/body/eval_jaxpr/ppermute | solution.py:10
  88.3 34.0 %collective-permute-start.2 = (bf16[128,4096]{1,0:T(8,128)(2,1)}, bf16[128,4096]{1,0:T(8,128)(2,1)}, u32[]{:S(2)}, u32[]{:S(2)}) collective-permute-start(bf16[128,4096]{1,0:T(8,128)(2,1)} %broadcast_select_fusion.3), channel_id=1, source_target_pairs={{16,0},{17,1},{18,2},{19,3},{20,4},{21,5},{22,6},{23,7},{24,8},{25... | collective-permute-start | bytes 3145736 | tf_op jit(solution)/shard_map/while/body/eval_jaxpr/ppermute | solution.py:10
  114.7 3.4 %copy-start.4 = (bf16[2,256,256]{2,1,0:T(8,128)(2,1)S(1)}, bf16[2,256,256]{2,1,0:T(8,128)(2,1)}, u32[]{:S(2)}) copy-start(bf16[2,256,256]{2,1,0:T(8,128)(2,1)} %get-tuple-element.145) | copy-start | bytes 786436 | tf_op jit(solution)/shard_map/cond
Sparse Core Ops, SparseCore 0:
  8.9 33.1 all-gather.1
where the time goes:
time: 131 us; the launch traced here: 130 us
  waiting for transfers between devices  84.8 us (65%)
  matrix products  14.5 us (11%)
  between operations  13.5 us (10%)
  starting transfers between devices  9.1 us (7%)
  other arithmetic  8.06 us (6%)
    ppermute x3, waiting for transfers between devices, from_behind(): return lax.ppermute(block, axis, route)  49.3 us
    all_gather x1, waiting for transfers between devices, per_device(): everyone = lax.all_gather(features, 'section', axis=1, tiled=True)  34.8 us
    ppermute x3, starting transfers between devices, from_behind(): return lax.ppermute(block, axis, route)  9.1 us
    dot_general x2, matrix products, cross_layer(): crossed = jnp.dot(blended, u_mat, preferred_element_type=jnp.float32)  7.47 us
    dot_general x2, matrix products, cross_layer(): projected = jnp.dot(current, v_mat, preferred_element_type=jnp.float32)  5.91 us
    select_n x3, other arithmetic, advance(): current = jnp.where(position == 0, anchor, incoming)  5.69 us
  transfers between devices with their start and end apart: 4, of which 3 were waited for; matrix products, arithmetic and copies ran while one was open for 9% of the time, Pallas kernels for 0%

commit v1 on v0

--- a/solution.py
+++ b/solution.py
@@ -40,7 +40,7 @@
     row_count = features.shape[2]
     feature_count = features.shape[3]
     piece_rows = row_count // pieces
-    everyone = lax.all_gather(features, "section", axis=1, tiled=True)
+    everyone = jnp.concatenate(lax.all_gather(features, "section"), axis=1)
     all_units = everyone.reshape(local_micro * section_count * pieces, piece_rows, feature_count)
     unit_count = all_units.shape[0]
     step_count = unit_count + section_count - 1

time: 131 us -> 131 us (level)
  no operation moved by 1% of the time
where the time goes in v1:
time: 131 us; the launch traced here: 130 us
  waiting for transfers between devices  84.8 us (65%)
  matrix products  14.5 us (11%)
  between operations  13.5 us (10%)
  starting transfers between devices  9.1 us (7%)
  other arithmetic  8.06 us (6%)
    ppermute x3, waiting for transfers between devices, from_behind(): return lax.ppermute(block, axis, route)  49.3 us
    all_gather x1, waiting for transfers between devices, per_device(): everyone = jnp.concatenate(lax.all_gather(features, 'section'), axis=1)  34.8 us
    ppermute x3, starting transfers between devices, from_behind(): return lax.ppermute(block, axis, route)  9.1 us
    dot_general x2, matrix products, cross_layer(): crossed = jnp.dot(blended, u_mat, preferred_element_type=jnp.float32)  7.47 us
    dot_general x2, matrix products, cross_layer(): projected = jnp.dot(current, v_mat, preferred_element_type=jnp.float32)  5.91 us
    select_n x3, other arithmetic, advance(): current = jnp.where(position == 0, anchor, incoming)  5.69 us
  transfers between devices with their start and end apart: 4, of which 3 were waited for; matrix products, arithmetic and copies ran while one was open for 9% of the time, Pallas kernels for 0%

profile of v1, /device:TPU:2, one launch (start us, length us, event | category | flops | bytes accessed | tf_op | source)
XLA Modules:
  0.0 130.4 jit_solution(2403684734066788996)
XLA Ops:
  6.5 0.0 copy-start
  6.5 0.0 copy-start.2
  6.5 0.0 copy-start.1
  6.5 0.0 all-gather.3.cloned.1.call-start
  6.5 0.7 all-gather.3.cloned.1.call-update
  7.3 34.8 %all-gather.3.cloned.1.call-done = bf16[2,1,128,4096]{3,2,1,0:T(8,128)(2,1)} async-done(((bf16[1,1,128,4096]{3,2,1,0:T(8,128)(2,1)}), bf16[2,1,128,4096]{3,2,1,0:T(8,128)(2,1)}) %all-gather.3.cloned.1.call-update) | async-done | bytes 2097168 | tf_op jit(solution)/shard_map/all_gather | solution.py:43
  42.1 1.4 %broadcast_select_fusion.2 = (bf16[128,4096]{1,0:T(8,128)(2,1)S(1)}, bf16[128,4096]{1,0:T(8,128)(2,1)S(1)}) fusion(pred[]{:T(512)S(6)} %eq.38, bf16[2,1,128,4096]{3,2,1,0:T(8,128)(2,1)} %all-gather.3.cloned.1.call-done, s32[]{:T(128)S(6)} %min.19), kind=kLoop, calls=%fused_computation.48 | loop fusion | flops 524288 | bytes 3145733 | tf_op jit(solution)/shard_map/while/body/eval_jaxpr/jit(_where)/select_n | solution.py:66
  43.5 0.0 copy-done
  43.5 0.0 copy-done.2
  43.5 0.0 copy-done.1
  43.5 1.3 collective-permute-start
  44.8 32.0 %collective-permute-done = bf16[128,4096]{1,0:T(8,128)(2,1)} collective-permute-done((bf16[128,4096]{1,0:T(8,128)(2,1)S(1)}, bf16[128,4096]{1,0:T(8,128)(2,1)}, u32[]{:S(2)}, u32[]{:S(2)}) %collective-permute-start) | collective-permute-done | bytes 1048608 | tf_op jit(solution)/shard_map/while/body/eval_jaxpr/ppermute | solution.py:10
  76.9 1.7 %broadcast_select_fusion.1 = (bf16[128,4096]{1,0:T(8,128)(2,1)S(1)}, bf16[128,4096]{1,0:T(8,128)(2,1)S(1)}) fusion(bf16[128,4096]{1,0:T(8,128)(2,1)} %collective-permute-done, pred[]{:T(512)S(6)} %eq.38, bf16[2,1,128,4096]{3,2,1,0:T(8,128)(2,1)} %all-gather.3.cloned.1.call-done, s32[]{:T(128)S(6)} %min.18), kind=kLoop, calls=%fused_computation.47 | loop fusion | flops 524288 | bytes 4194309 | tf_op jit(solution)/shard_map/while/body/eval_jaxpr/jit(_where)/select_n | solution.py:66
  78.5 7.3 %conditional.4 = (bf16[128,4096]{1,0:T(8,128)(2,1)S(1)}) conditional(s32[]{:T(128)} %convert_element_type.57, bf16[128,4096]{1,0:T(8,128)(2,1)S(1)} %get-tuple-element.150, (bf16[128,4096]{1,0:T(8,128)(2,1)S(1)}, bf16[128,4096]{1,0:T(8,128)(2,1)S(1)}, bf16[2,4096]{1,0:T(2,128)(2,1)S(1)}, bf16[4096,512]{1,0:T(8,128)(2,1)}, ...), branch_computations={%region_3.4_spmd, %region_4.6_spmd} | conditional | flops 1112736768 | bytes 15767588 | solution.py:67
  78.5 0.0 copy-start.3
  78.6 3.0 %fusion.14 = bf16[128,512]{1,0:T(8,128)(2,1)S(1)} fusion(bf16[128,4096]{1,0:T(8,128)(2,1)S(1)} %get-tuple-element.134, bf16[4096,512]{1,0:T(8,128)(2,1)} %get-tuple-element.137), kind=kOutput, calls=%fused_computation.22 | convolution fusion | flops 536936448 | bytes 5373952 | tf_op jit(solution)/shard_map/while/body/eval_jaxpr/cond/branch_1_fun/dot_general | solution.py:17
  81.5 0.4 fusion.28
  82.0 0.0 copy-done.3
  82.0 0.2 fusion.15
  82.2 0.1 copy.43
  82.3 3.6 %fusion.11 = bf16[128,4096]{1,0:T(8,128)(2,1)S(1)} fusion(bf16[128,512]{0,1:T(8,128)(2,1)S(1)} %bitcast.79, bf16[512,4096]{1,0:T(8,128)(2,1)} %get-tuple-element.139, bf16[128,4096]{1,0:T(8,128)(2,1)S(1)} %get-tuple-element.135, bf16[128,4096]{1,0:T(8,128)(2,1)S(1)} %get-tuple-element.134, f32[4096]{0:T(1024)S(1)} %bitcast.85), kind=kOutput, calls=%fused_computation.17 | convolution fusion | flops 540016640 | bytes 7487488 | tf_op jit(solution)/shard_map/while/body/eval_jaxpr/cond/branch_1_fun/dot_general | solution.py:30
  85.9 1.3 collective-permute-start.1
  87.2 1.1 broadcast_select_fusion.3
  88.3 6.5 %collective-permute-start.2 = (bf16[128,4096]{1,0:T(8,128)(2,1)}, bf16[128,4096]{1,0:T(8,128)(2,1)}, u32[]{:S(2)}, u32[]{:S(2)}) collective-permute-start(bf16[128,4096]{1,0:T(8,128)(2,1)} %broadcast_select_fusion.3), channel_id=1, source_target_pairs={{16,0},{17,1},{18,2},{19,3},{20,4},{21,5},{22,6},{23,7},{24,8},{25... | collective-permute-start | bytes 3145736 | tf_op jit(solution)/shard_map/while/body/eval_jaxpr/ppermute | solution.py:10
  94.8 17.2 %collective-permute-done.1 = bf16[128,4096]{1,0:T(8,128)(2,1)} collective-permute-done((bf16[128,4096]{1,0:T(8,128)(2,1)S(1)}, bf16[128,4096]{1,0:T(8,128)(2,1)}, u32[]{:S(2)}, u32[]{:S(2)}) %collective-permute-start.1) | collective-permute-done | bytes 1048608 | tf_op jit(solution)/shard_map/while/body/eval_jaxpr/ppermute | solution.py:10
  112.0 2.6 %broadcast_select_fusion = (bf16[128,4096]{1,0:T(8,128)(2,1)S(1)}, bf16[128,4096]{1,0:T(8,128)(2,1)}) fusion(bf16[128,4096]{1,0:T(8,128)(2,1)} %collective-permute-done.1, pred[]{:T(512)S(6)} %eq.38, bf16[2,1,128,4096]{3,2,1,0:T(8,128)(2,1)} %all-gather.3.cloned.1.call-done, s32[]{:T(128)S(6)} %min.17), kind=kLoop, calls=%fused_computation.46 | loop fusion | flops 524288 | bytes 4194309 | tf_op jit(solution)/shard_map/jit(_where)/select_n | solution.py:66
  114.7 7.6 %conditional.5 = (bf16[128,4096]{1,0:T(8,128)(2,1)S(1)}) conditional(s32[]{:T(128)} %convert_element_type.56, bf16[128,4096]{1,0:T(8,128)(2,1)S(1)} %get-tuple-element.148, (bf16[128,4096]{1,0:T(8,128)(2,1)S(1)}, bf16[128,4096]{1,0:T(8,128)(2,1)}, bf16[2,4096]{1,0:T(2,128)(2,1)S(1)}, bf16[4096,512]{1,0:T(8,128)(2,1)}, bf16[2,256,256]{2,1,0:T(8,128)(2,1)}, ...), branch_computations={%region_6.7_spmd, %region_7.9_spmd} | conditional | flops 1112736768 | bytes 15767588 | solution.py:67
  114.7 0.0 copy-start.4
  114.7 3.0 %fusion.23 = bf16[128,512]{1,0:T(8,128)(2,1)S(1)} fusion(bf16[128,4096]{1,0:T(8,128)(2,1)S(1)} %get-tuple-element.141, bf16[4096,512]{1,0:T(8,128)(2,1)} %get-tuple-element.144), kind=kOutput, calls=%fused_computation.36 | convolution fusion | flops 536936448 | bytes 5373952 | tf_op jit(solution)/shard_map/cond/branch_1_fun/dot_general | solution.py:17
  117.7 0.4 fusion.29
  118.1 0.0 copy-done.4
  118.1 0.2 fusion.24
  118.3 0.1 copy.45
  118.4 3.9 %fusion.20 = bf16[128,4096]{1,0:T(8,128)(2,1)S(1)} fusion(bf16[128,512]{0,1:T(8,128)(2,1)S(1)} %bitcast.80, bf16[512,4096]{1,0:T(8,128)(2,1)} %get-tuple-element.146, bf16[128,4096]{1,0:T(8,128)(2,1)} %get-tuple-element.142, bf16[128,4096]{1,0:T(8,128)(2,1)S(1)} %get-tuple-element.141, f32[4096]{0:T(1024)S(1)} %bitcast.86), kind=kOutput, calls=%fused_computation.31 | convolution fusion | flops 540016640 | bytes 7487488 | tf_op jit(solution)/shard_map/cond/branch_1_fun/dot_general | solution.py:30
  122.3 0.0 collective-permute-done.2
  122.3 1.2 select_bitcast_fusion
  (5 shorter events, 0.1 us)
Async XLA Ops:
  6.5 36.9 %copy-start = (bf16[1,2,4096]{2,1,0:T(2,128)(2,1)S(1)}, bf16[1,2,4096]{2,1,0:T(2,128)(2,1)}, u32[]{:S(2)}) copy-start(bf16[1,2,4096]{2,1,0:T(2,128)(2,1)} %param.16) | copy-start | bytes 49156
  6.5 36.9 %copy-start.2 = (bf16[1,2,256,256]{3,2,1,0:T(8,128)(2,1)S(1)}, bf16[1,2,256,256]{3,2,1,0:T(8,128)(2,1)}, u32[]{:S(2)}) copy-start(bf16[1,2,256,256]{3,2,1,0:T(8,128)(2,1)} %param.14) | copy-start | bytes 786436
  6.5 37.0 %copy-start.1 = (f32[1,4096]{1,0:T(1,128)S(1)}, f32[1,4096]{1,0:T(1,128)}, u32[]{:S(2)}) copy-start(f32[1,4096]{1,0:T(1,128)} %param.17) | copy-start | bytes 49156
  6.5 35.6 %all-gather.3.cloned.1.call-start = ((), (), s32[]{:S(2)}) async-start(), calls=%async_computation | async-start | bytes 3145728 | tf_op jit(solution)/shard_map/all_gather | solution.py:43
  43.5 33.3 %collective-permute-start = (bf16[128,4096]{1,0:T(8,128)(2,1)S(1)}, bf16[128,4096]{1,0:T(8,128)(2,1)}, u32[]{:S(2)}, u32[]{:S(2)}) collective-permute-start(bf16[128,4096]{1,0:T(8,128)(2,1)S(1)} %get-tuple-element.154), channel_id=1, source_target_pairs={{0,16},{1,17},{2,18},{3,19},{4,20},{5,21},{6,22},{7,23},{8,24},{9,... | collective-permute-start | bytes 3145736 | tf_op jit(solution)/shard_map/while/body/eval_jaxpr/ppermute | solution.py:10
  78.5 3.4 %copy-start.3 = (bf16[2,256,256]{2,1,0:T(8,128)(2,1)S(1)}, bf16[2,256,256]{2,1,0:T(8,128)(2,1)}, u32[]{:S(2)}) copy-start(bf16[2,256,256]{2,1,0:T(8,128)(2,1)} %get-tuple-element.138) | copy-start | bytes 786436 | tf_op jit(solution)/shard_map/while/body/eval_jaxpr/cond
  85.9 26.2 %collective-permute-start.1 = (bf16[128,4096]{1,0:T(8,128)(2,1)S(1)}, bf16[128,4096]{1,0:T(8,128)(2,1)}, u32[]{:S(2)}, u32[]{:S(2)}) collective-permute-start(bf16[128,4096]{1,0:T(8,128)(2,1)S(1)} %get-tuple-element.155), channel_id=1, source_target_pairs={{0,16},{1,17},{2,18},{3,19},{4,20},{5,21},{6,22},{7,23},{8,24},{9,... | collective-permute-start | bytes 3145736 | tf_op jit(solution)/shard_map/while/body/eval_jaxpr/ppermute | solution.py:10
  88.3 34.0 %collective-permute-start.2 = (bf16[128,4096]{1,0:T(8,128)(2,1)}, bf16[128,4096]{1,0:T(8,128)(2,1)}, u32[]{:S(2)}, u32[]{:S(2)}) collective-permute-start(bf16[128,4096]{1,0:T(8,128)(2,1)} %broadcast_select_fusion.3), channel_id=1, source_target_pairs={{16,0},{17,1},{18,2},{19,3},{20,4},{21,5},{22,6},{23,7},{24,8},{25... | collective-permute-start | bytes 3145736 | tf_op jit(solution)/shard_map/while/body/eval_jaxpr/ppermute | solution.py:10
  114.7 3.4 %copy-start.4 = (bf16[2,256,256]{2,1,0:T(8,128)(2,1)S(1)}, bf16[2,256,256]{2,1,0:T(8,128)(2,1)}, u32[]{:S(2)}) copy-start(bf16[2,256,256]{2,1,0:T(8,128)(2,1)} %get-tuple-element.145) | copy-start | bytes 786436 | tf_op jit(solution)/shard_map/cond
Sparse Core Ops, SparseCore 0:
  8.9 33.1 all-gather.2
